TPU v7x, 256 devices: a whole 4x4x8 slice. The times are simulated.
256 devices in a mesh: pair: 128 (over x_hi, z, y, core), ao: 2 (over x_lo).
Axes of the slice: x: 4 (x_hi: 2, x_lo: 2; x = x_hi * 2 + x_lo), y: 4, z: 8, core: 2. Of those that a mesh axis runs over, the one named last changes fastest.
Arguments:
- gamma: bfloat16 [128, 1792, 1792], P('pair', 'ao'), may hold values from -6 to 6
- c_vir: bfloat16 [1024, 1792], replicated, may hold values from -0.125 to 0.125
- c_occ: bfloat16 [1024, 256], replicated, may hold values from -1.796875 to 1.796875
- pair_list: int32 [128, 2], replicated, may hold values from 0 to 255
- shell_order: int32 [128], replicated, may hold values from 0 to 127, each once
Outputs:
- ao_density: bfloat16 [1024, 1024], P('ao', 'pair')
Inputs may be any that keep to these rules, and one draw needn't show every extreme that they name: shell_order holds each of 0 to 127 once.
All inputs are finite; a program needn't handle non-finite values.
Results may differ from a plain program's by a relative error of at most 0.0049.
Values sent between devices are 32-bit elements; how exact they have to be, the bound alone decides.
A program may use at most 64 MiB of HBM per device.

v0:
```python
import jax
import jax.numpy as jnp
from jax import lax
from jax.sharding import PartitionSpec as P

SB = 8


def cut_along(x, dim, length):
    dims = x.shape
    tiles = x.reshape(*dims[:dim], length, dims[dim] // length, *dims[dim + 1 :])
    return jnp.moveaxis(tiles, dim, 0)


def sent_and_summed(x, axis, dim):
    length = lax.axis_size(axis)
    tiles = lax.all_to_all(cut_along(x, dim, length), axis, 0, 0, tiled=True)
    return jnp.sum(tiles, axis=0)


def shards(gamma, c_vir, c_occ, pair_list, shell_order):
    basis = c_vir.shape[0]
    groups = lax.axis_size("pair")
    own_index = lax.axis_index("pair")
    ao_index = lax.axis_index("ao")
    ao_count = lax.axis_size("ao")
    amplitude = gamma[0]
    local_vir = amplitude.shape[0]
    offsets = jnp.arange(SB, dtype=jnp.int32)
    row_index = (shell_order[:, None] * SB + offsets[None, :]).reshape(-1)
    vir_sorted = lax.dynamic_slice_in_dim(c_vir[row_index], ao_index * local_vir, local_vir, 1)
    half_block = lax.dot_general(
        amplitude, c_vir, (((1,), (1,)), ((), ())), preferred_element_type=jnp.float32
    ).astype(jnp.bfloat16)
    owned = basis // groups
    width_nu = basis // ao_count
    my_rows = lax.dynamic_slice_in_dim(row_index, own_index * owned, owned)
    nu_rows = ao_index * width_nu + jnp.arange(width_nu, dtype=jnp.int32)
    summed = sent_and_summed(
        lax.dot_general(
            half_block, vir_sorted, (((0,), (1,)), ((), ())), preferred_element_type=jnp.float32
        ),
        "ao",
        0,
    )
    blocks = lax.all_to_all(summed, "pair", split_axis=1, concat_axis=1, tiled=True)
    values = blocks.reshape(width_nu, groups, owned)
    left_weight = c_occ[my_rows][:, pair_list[:, 0]].astype(jnp.float32)
    right_weight = c_occ[nu_rows][:, pair_list[:, 1]].astype(jnp.float32)
    result = jnp.einsum("np,npr,rp->nr", right_weight, values, left_weight)
    return result.astype(jnp.bfloat16)


def solution(mesh):
    return jax.shard_map(
        shards,
        mesh=mesh,
        in_specs=(P("pair", "ao", None), P(), P(), P(), P()),
        out_specs=P("ao", "pair"),
        check_vma=False,
    )
```

profile of v0, /device:TPU:1, one launch (start us, length us, event | category | flops | bytes accessed | tf_op | source)
XLA Modules:
  0.0 158.2 jit_solution(15369253426494974241)
XLA Ops:
  0.0 0.0 copy-start
  0.0 0.8 broadcast_multiply_fusion
  0.8 0.1 iota_add_fusion
  0.9 0.1 add.91
  1.0 10.4 %gather_fusion.2 = bf16[1024,1792]{1,0:T(8,128)(2,1)} fusion(bf16[1024,1792]{1,0:T(8,128)(2,1)} %param.6, s32[1024]{0:T(1024)S(1)} %broadcast_clamp_fusion), kind=kCustom, calls=%fused_computation.2 | custom fusion | bytes 7344128 | tf_op jit(solution)/shard_map/gather | solution.py:31
  11.5 0.0 copy-done
  11.5 10.2 %fusion.5 = f32[1024,1024]{1,0:T(8,128)} fusion(bf16[1024,1792]{1,0:T(8,128)(2,1)} %gather_fusion.2, s32[]{:T(128)S(6)} %select_n.40, bf16[1024,1792]{1,0:T(8,128)(2,1)} %param.6, bf16[1,896,1792]{2,1,0:T(8,128)(2,1)S(1)} %copy-done), kind=kOutput, calls=%fused_computation.11 | convolution fusion | flops 5168300032 | bytes 12910596 | tf_op jit(solution)/shard_map/dot_general | solution.py:40
  21.7 52.8 %all_to_all.14 = f32[2,512,1024]{2,1,0:T(8,128)} all-to-all(f32[2,512,1024]{2,1,0:T(8,128)} %bitcast.35), channel_id=1, replica_groups=mesh['pair'=128,'ao'=2] {'ao'}, dimensions={0} | all-to-all | bytes 8388608 | tf_op jit(solution)/shard_map/all_to_all | solution.py:17
  74.5 4.1 %reduce_sum.9 = f32[512,1024]{1,0:T(8,128)} reduce(f32[2,512,1024]{2,1,0:T(8,128)} %all_to_all.14, f32[]{:T(128)} %constant.18.clone.1), dimensions={0}, to_apply=%region_0.0 | reduce | flops 524288 | bytes 6291460 | tf_op jit(solution)/shard_map/reduce_sum | solution.py:18
  78.6 2.9 %copy.11 = f32[512,1024]{0,1:T(8,128)} copy(f32[512,1024]{1,0:T(8,128)} %reduce_sum.9) | data formatting | bytes 4194304 | tf_op jit(solution)/shard_map/reduce_sum | solution.py:18
  81.5 0.0 copy-start.1
  81.5 19.2 %all-to-all-start.1 = ((f32[512,128,8]{0,2,1:T(8,128)}), f32[512,128,8]{0,2,1:T(8,128)}, u32[]{:S(2)}, u32[]{:S(2)}) async-start(f32[512,128,8]{0,2,1:T(8,128)} %bitcast.34), calls=%async_computation.1 | async-start | bytes 4194304 | tf_op jit(solution)/shard_map/all_to_all | solution.py:46
  100.7 0.1 add.95
  100.8 0.1 compare_select_fusion.3
  100.9 1.7 %gather_fusion.3 = bf16[8,256]{1,0:T(8,128)(2,1)S(1)} fusion(bf16[1024,256]{1,0:T(8,128)(2,1)} %param.7, s32[1024]{0:T(1024)S(1)} %pad_clamp_fusion.1), kind=kCustom, calls=%fused_computation.3 | custom fusion | bytes 8224 | tf_op jit(solution)/shard_map/gather | solution.py:48
  102.6 0.1 copy.12
  102.7 3.3 %gather_fusion = bf16[512,256]{1,0:T(8,128)(2,1)} fusion(bf16[1024,256]{1,0:T(8,128)(2,1)} %param.7, s32[1024]{0:T(1024)S(1)} %pad_clamp_fusion.3), kind=kCustom, calls=%fused_computation | custom fusion | bytes 526336 | tf_op jit(solution)/shard_map/gather | solution.py:49
  106.0 1.1 copy.10
  107.1 0.0 copy-done.1
  107.2 1.3 gather_fusion.4
  108.5 1.5 gather_fusion.1
  110.0 0.8 convert_bitcast_fusion
  110.7 0.9 bitcast_convert_fusion
  111.7 44.1 %all-to-all-done.1 = f32[512,128,8]{0,2,1:T(8,128)} async-done(((f32[512,128,8]{0,2,1:T(8,128)}), f32[512,128,8]{0,2,1:T(8,128)}, u32[]{:S(2)}, u32[]{:S(2)}) %all-to-all-start.1) | async-done | bytes 2097184 | tf_op jit(solution)/shard_map/all_to_all | solution.py:46
  155.7 2.5 %fusion.4 = bf16[512,8]{0,1:T(8,128)(2,1)} fusion(f32[512,128,8]{0,2,1:T(8,128)} %all-to-all-done.1, f32[512,128]{0,1:T(8,128)S(1)} %bitcast_convert_fusion, f32[8,128]{0,1:T(8,128)S(1)} %convert_bitcast_fusion), kind=kLoop, calls=%fused_computation.10 | loop fusion | flops 1568768 | bytes 2371584 | tf_op jit(solution)/shard_map/np,npr,rp->nr/dot_general | solution.py:50
  (7 shorter events, 0.0 us)
Async XLA Ops:
  0.0 11.5 %copy-start = (bf16[1,896,1792]{2,1,0:T(8,128)(2,1)S(1)}, bf16[1,896,1792]{2,1,0:T(8,128)(2,1)}, u32[]{:S(2)}) copy-start(bf16[1,896,1792]{2,1,0:T(8,128)(2,1)} %param.5) | copy-start | bytes 9633796
  81.5 25.6 %copy-start.1 = (s32[128,2]{0,1:T(2,128)S(1)}, s32[128,2]{0,1:T(2,128)}, u32[]{:S(2)}) copy-start(s32[128,2]{0,1:T(2,128)} %param.8) | copy-start | bytes 3076
  81.5 74.2 %all-to-all-start.1 = ((f32[512,128,8]{0,2,1:T(8,128)}), f32[512,128,8]{0,2,1:T(8,128)}, u32[]{:S(2)}, u32[]{:S(2)}) async-start(f32[512,128,8]{0,2,1:T(8,128)} %bitcast.34), calls=%async_computation.1 | async-start | bytes 4194304 | tf_op jit(solution)/shard_map/all_to_all | solution.py:46
where the time goes:
time: 159 us; the launch traced here: 158 us
  blocking collectives  52.8 us (33%)
  waiting for transfers between devices  44.1 us (28%)
  local copies, waits for them, and re-layouts  22.6 us (14%)
  starting transfers between devices  19.2 us (12%)
  matrix products  10.2 us (6%)
  other arithmetic  9.26 us (6%)
    all_to_all x1, blocking collectives, sent_and_summed(): tiles = lax.all_to_all(cut_along(x, dim, length), axis, 0, 0, tiled=True)  52.8 us
    all_to_all x1, waiting for transfers between devices, shards(): lax.all_to_all(summed, 'pair', split_axis=1, concat_axis=1, tiled=True)  44.1 us
    all_to_all x1, starting transfers between devices, shards(): lax.all_to_all(summed, 'pair', split_axis=1, concat_axis=1, tiled=True)  19.2 us
    gather x1, local copies, waits for them, and re-layouts, shards(): c_vir[row_index]  10.4 us
    dot_general x1, matrix products, shards(): lax.dot_general(half_block, vir_sorted, (((0,), (1,)), ((), ())), preferr...  10.2 us
    gather x3, local copies, waits for them, and re-layouts, shards(): right_weight = c_occ[nu_rows][:, pair_list[:, 1]].astype(jnp.float32)  5.89 us
    reduce_sum x1, other arithmetic, sent_and_summed(): return jnp.sum(tiles, axis=0)  4.09 us
  transfers between devices with their start and end apart: 1, of which 1 were waited for; matrix products, arithmetic and copies ran while one was open for 7% of the time, Pallas kernels for 0%

commit v1 on v0

v1 whole, which is shorter than its diff:
```python
import jax
import jax.numpy as jnp
from jax import lax
from jax.experimental import pallas as pl
from jax.experimental.pallas import tpu as pltpu
from jax.sharding import PartitionSpec as P

MESH = pl.DeviceIdType.MESH
SB = 8
XS, YS, ZS = 4, 4, 8
NCH = 4
LANES = 128


def kernel(gamma, c_vir, c_occ, pairs, shells, out, g, cv, co, pair_s, shell_s,
           lw, rw, half, block, s_buf, r_d, r_1, r_2, r_3, c_buf, r_z,
           in_sem, d_send, d_recv, send_1, recv_1, send_2, recv_2, send_3, recv_3, send_z, recv_z):
    local, vir = g.shape
    basis = cv.shape[0]
    pair = lax.axis_index("pair")
    xlo = lax.axis_index("ao")
    core = pair % 2
    y = (pair // 2) % YS
    z = (pair // (2 * YS)) % ZS
    xhi = pair // (2 * YS * ZS)
    yhi, ylo = y // 2, y % 2

    def device(xh, xl, yy, zz, cc):
        return (((xh * ZS + zz) * YS + yy) * 2 + cc, xl)

    def relative(hi, lo, a, b, c):
        own = (hi + lo * (1 - c)) % 2
        low = (lo + b) % 2
        return ((own + a) % 2 + low * (1 - c)) % 2, low

    def x_peer(a, b):
        hi, lo = relative(xhi, xlo, a, b, core)
        return device(hi, lo, y, z, core)

    def y_peer(a, b):
        hi, lo = relative(yhi, ylo, a, b, core)
        return device(xhi, xlo, hi * 2 + lo, z, core)

    def z_peer(dz):
        return device(xhi, xlo, y, (z + dz) % ZS, core)

    twin = device(xhi, xlo, y, z, 1 - core)
    x_first = device((xhi + core) % 2, 1 - xlo, y, z, core)
    y_first = device(xhi, xlo, ((yhi + core) % 2) * 2 + (1 - ylo), z, core)
    x_second = x_peer(0, 1)
    y_second = y_peer(0, 1)

    own_half = xlo * (basis // 2)
    other_half = (1 - xlo) * (basis // 2)

    def row_starts(j):
        return (pl.multiple_of(own_half + j * LANES, LANES), pl.multiple_of(other_half + j * LANES, LANES))

    copies = {}

    def load(name, src, dst, k):
        copies[name] = pltpu.make_async_copy(src, dst, in_sem.at[k])
        copies[name].start()

    load("shell", shells, shell_s, 0)
    load("pair", pairs, pair_s, 1)
    count = 2
    mid = local // 2
    for t, start in enumerate(row_starts(0)):
        load(("cv", 0, t), c_vir.at[pl.ds(start, LANES)], cv.at[pl.ds(start, LANES)], count)
        count += 1
    for t in range(2):
        load(("g", t), gamma.at[0, pl.ds(t * mid, mid)], g.at[pl.ds(t * mid, mid)], count)
        count += 1
    load("co", c_occ, co, count)
    count += 1
    for j in range(1, NCH):
        for t, start in enumerate(row_starts(j)):
            load(("cv", j, t), c_vir.at[pl.ds(start, LANES)], cv.at[pl.ds(start, LANES)], count)
            count += 1

    barrier = pltpu.get_barrier_semaphore()
    peers = [twin]
    peers += [x_peer(a, b) for a, b in ((0, 1), (1, 0), (1, 1))]
    peers += [y_peer(a, b) for a, b in ((0, 1), (1, 0), (1, 1))]
    peers += [z_peer(dz) for dz in range(1, ZS)]
    for peer in peers:
        pl.semaphore_signal(barrier, inc=1, device_id=peer, device_id_type=MESH)

    copies["shell"].wait()
    bits = [(a, b) for a in range(2) for b in range(2)]
    z_part = [((z + dz) % ZS) * (2 * YS) for dz in range(ZS)]
    x_part, y_part = {}, {}
    for d in range(2):
        cc = (core + d) % 2
        for a, b in bits:
            hi, lo = relative(xhi, xlo, a, b, cc)
            x_part[d, a, b] = hi * (2 * YS * ZS) + cc
            hi, lo = relative(yhi, ylo, a, b, cc)
            y_part[d, a, b] = (hi * 2 + lo) * 2

    def weights():
        copies["pair"].wait()
        copies["co"].wait()
        left = pair_s[0, pair]
        right = pair_s[1, pair]
        occ = co.shape[1]
        pick = jnp.where(lax.broadcasted_iota(jnp.int32, (occ, LANES), 0) == left, 1.0, 0.0).astype(jnp.bfloat16)
        lw[...] = jnp.dot(co[...], pick, preferred_element_type=jnp.float32).reshape(lw.shape)
        pick = jnp.where(lax.broadcasted_iota(jnp.int32, (16, occ), 1) == right, 1.0, 0.0).astype(jnp.bfloat16)
        rw[...] = lax.dot_general(pick, co[...], (((1,), (1,)), ((), ())), preferred_element_type=jnp.float32)[:8]

    def compute_half(j):
        starts = row_starts(j)
        rhs = jnp.concatenate([cv[pl.ds(start, LANES), :] for start in starts], axis=0)
        for t in range(2):
            if j == 0:
                copies["g", t].wait()
            half[pl.ds(t * mid, mid), :] = lax.dot_general(
                g[pl.ds(t * mid, mid), :], rhs, (((1,), (1,)), ((), ())), preferred_element_type=jnp.float32
            ).astype(jnp.bfloat16)

    def compute_block(j):
        column = pl.multiple_of(xlo * local, LANES)
        tall = basis // 2
        for t in range(2):
            block[pl.ds(t * tall // SB, tall // SB)] = jnp.dot(
                cv[pl.ds(t * tall, tall), pl.ds(column, local)], half[...], preferred_element_type=jnp.float32
            ).reshape(tall // SB, SB, 2 * LANES)

    def remote(src, dst, send, recv, peer):
        return pltpu.make_async_remote_copy(
            src_ref=src, dst_ref=dst, send_sem=send, recv_sem=recv, device_id=peer, device_id_type=MESH)

    def copy_d(j):
        return remote(s_buf.at[j, 1], r_d.at[j], d_send.at[j], d_recv.at[j], twin)

    def copy_1(j, part):
        return remote(s_buf.at[j, 0, part, pl.ds(32, 32)], r_1.at[j, part], send_1.at[j, part], recv_1.at[j, part],
                      (x_first, y_first)[part])

    def copy_2(j, part):
        return remote(s_buf.at[j, 0, part, pl.ds(16, 16)], r_2.at[j, part], send_2.at[j, part], recv_2.at[j, part],
                      (x_second, y_second)[part])

    def copy_3(j, part, t):
        a, b = bits[t]
        return remote(s_buf.at[j, 0, part, pl.ds(t * 4, 4)], r_3.at[j, part, t - 1], send_3.at[j, part, t - 1],
                      recv_3.at[j, part, t - 1], (y_peer if part == 0 else x_peer)(a, b))

    def copy_z(j, dz):
        return remote(c_buf.at[j, dz], r_z.at[j, dz - 1], send_z.at[j, dz - 1], recv_z.at[j, dz - 1], z_peer(dz))

    def weigh(j):
        right = [rw[:, pl.ds(start, LANES)] for start in row_starts(j)]
        for d in (1, 0):
            for part in range(2):
                for u in range(4):
                    for v in range(4):
                        xb, yb = (bits[u], bits[v]) if part == 0 else (bits[v], bits[u])
                        xy = x_part[(d,) + xb] + y_part[(d,) + yb]
                        b = xb[1]
                        for w in range(4):
                            shell = shell_s[xy + z_part[part * 4 + w]]
                            tile = block[shell, :, b * LANES : (b + 1) * LANES] * right[b]
                            s_buf[j, d, part, (u * 4 + v) * 4 + w] = tile * lw[shell]
            if d == 1:
                copy_d(j).start()

    def stage_c(j):
        if j == 0:
            for t in range(2):
                copies["cv", 0, t].wait()
        compute_half(j)
        if j == 0:
            for k in range(1, NCH):
                for t in range(2):
                    copies["cv", k, t].wait()
            weights()
        compute_block(j)
        if j == 0:
            pl.semaphore_wait(barrier, len(peers))
        weigh(j)

    def stage_e(j):
        copy_d(j).wait_recv()
        for part in range(2):
            s_buf[j, 0, part, pl.ds(32, 32)] = s_buf[j, 0, part, pl.ds(32, 32)] + r_d[j, part, pl.ds(32, 32)]
            copy_1(j, part).start()
        for part in range(2):
            s_buf[j, 0, part, pl.ds(0, 32)] = s_buf[j, 0, part, pl.ds(0, 32)] + r_d[j, part, pl.ds(0, 32)]

    def stage_f(j):
        for part in range(2):
            copy_1(j, part).wait_recv()
            s_buf[j, 0, part, pl.ds(16, 16)] = s_buf[j, 0, part, pl.ds(16, 16)] + r_1[j, part, pl.ds(0, 16)]
            copy_2(j, part).start()
            s_buf[j, 0, part, pl.ds(0, 16)] = s_buf[j, 0, part, pl.ds(0, 16)] + r_1[j, part, pl.ds(16, 16)]

    def stage_g(j):
        for part in range(2):
            copy_2(j, part).wait_recv()
            s_buf[j, 0, part, pl.ds(0, 16)] = s_buf[j, 0, part, pl.ds(0, 16)] + r_2[j, part]
            for t in (3, 2, 1):
                copy_3(j, part, t).start()

    def stage_h(j):
        for part in range(2):
            total = s_buf[j, 0, part, pl.ds(0, 4)]
            for t in (1, 2, 3):
                copy_3(j, part, t).wait_recv()
                total = total + r_3[j, part, t - 1]
            c_buf[j, pl.ds(part * 4, 4)] = total
        for dz in (4, 3, 5, 2, 6, 1, 7):
            copy_z(j, dz).start()

    def stage_i(j):
        total = c_buf[j, 0]
        for dz in range(1, ZS):
            copy_z(j, dz).wait_recv()
            total = total + r_z[j, dz - 1]
        out[:, j * LANES : (j + 1) * LANES] = total

    order = (stage_c, 0), (stage_c, 1), (stage_e, 0), (stage_c, 2), (stage_e, 1), (stage_c, 3), (stage_e, 2), (stage_f, 0)
    order += (stage_e, 3), (stage_f, 1), (stage_g, 0), (stage_f, 2), (stage_g, 1), (stage_f, 3), (stage_h, 0), (stage_g, 2)
    order += (stage_h, 1), (stage_g, 3), (stage_h, 2), (stage_i, 0), (stage_h, 3), (stage_i, 1), (stage_i, 2), (stage_i, 3)
    for stage, j in order:
        stage(j)
    for j in range(NCH):
        copy_d(j).wait_send()
        for part in range(2):
            copy_1(j, part).wait_send()
            copy_2(j, part).wait_send()
            for t in (1, 2, 3):
                copy_3(j, part, t).wait_send()
        for dz in range(1, ZS):
            copy_z(j, dz).wait_send()


def shards(gamma, c_vir, c_occ, pair_list, shell_order):
    local, vir = gamma.shape[1:]
    basis = c_vir.shape[0]
    f32, bf16 = jnp.float32, jnp.bfloat16
    dma = pltpu.SemaphoreType.DMA
    tile = (SB, LANES)
    summed = pl.pallas_call(
        kernel,
        out_shape=jax.ShapeDtypeStruct((SB, basis // 2), f32),
        in_specs=[pl.BlockSpec(memory_space=pl.ANY)] * 5,
        out_specs=pl.BlockSpec(memory_space=pltpu.VMEM),
        scratch_shapes=[
            pltpu.VMEM((local, vir), bf16),
            pltpu.VMEM((basis, vir), bf16),
            pltpu.VMEM(c_occ.shape, bf16),
            pltpu.SMEM((2, pair_list.shape[0]), jnp.int32),
            pltpu.SMEM(shell_order.shape, jnp.int32),
            pltpu.VMEM((basis // SB, SB, LANES), f32),
            pltpu.VMEM((8, basis), f32),
            pltpu.VMEM((local, 2 * LANES), bf16),
            pltpu.VMEM((basis // SB, SB, 2 * LANES), f32),
            pltpu.VMEM((NCH, 2, 2, 64) + tile, f32),
            pltpu.VMEM((NCH, 2, 64) + tile, f32),
            pltpu.VMEM((NCH, 2, 32) + tile, f32),
            pltpu.VMEM((NCH, 2, 16) + tile, f32),
            pltpu.VMEM((NCH, 2, 3, 4) + tile, f32),
            pltpu.VMEM((NCH, ZS) + tile, f32),
            pltpu.VMEM((NCH, ZS - 1) + tile, f32),
            dma((13,)),
            dma((NCH,)), dma((NCH,)),
            dma((NCH, 2)), dma((NCH, 2)),
            dma((NCH, 2)), dma((NCH, 2)),
            dma((NCH, 2, 3)), dma((NCH, 2, 3)),
            dma((NCH, ZS - 1)), dma((NCH, ZS - 1)),
        ],
        compiler_params=pltpu.CompilerParams(
            collective_id=0, has_side_effects=True, vmem_limit_bytes=60 * 1024 * 1024),
        name="density",
    )(gamma, c_vir, c_occ, pair_list.T, shell_order)
    return summed.T.astype(bf16)


def solution(mesh):
    return jax.shard_map(
        shards,
        mesh=mesh,
        in_specs=(P("pair", "ao", None), P(), P(), P(), P()),
        out_specs=P("ao", "pair"),
        check_vma=False,
    )
```

time: 159 us -> 40.6 us (0.26)
  the two profiles are of different devices: /device:TPU:1 before, /device:TPU:32 now
where the time goes in v1:
time: 40.6 us; the launch traced here: 40.4 us
  Pallas kernels  39.1 us (96%)
  other arithmetic  1.32 us (3%)
    pallas_call x1, Pallas kernels, shards(): pl.pallas_call(kernel, out_shape=jax.ShapeDtypeStruct((SB, basis // 2), f...  39.1 us
    convert_element_type x1, other arithmetic, shards(): return summed.T.astype(bf16)  1.32 us

profile of v1, /device:TPU:32, one launch (start us, length us, event | category | flops | bytes accessed | tf_op | source)
XLA Modules:
  0.0 40.4 jit_solution(16727800452970577890)
XLA Ops:
  0.0 39.1 %density.1 = f32[8,512]{1,0:T(8,128)} custom-call(bf16[1,896,1792]{2,1,0:T(8,128)(2,1)} %gamma.1, bf16[1024,1792]{1,0:T(8,128)(2,1)} %c_vir.1, bf16[1024,256]{1,0:T(8,128)(2,1)} %c_occ.1, s32[2,128]{1,0:T(2,128)} %bitcast.3, s32[128]{0:T(128)} %shells.1), custom_call_target="tpu_custom_call" | custom-call | tf_op jit(solution)/shard_map/density/pallas_call | solution.py:246
  39.1 1.3 %convert_bitcast_fusion = bf16[512,8]{0,1:T(8,128)(2,1)} fusion(f32[8,512]{1,0:T(8,128)} %density.1), kind=kLoop, calls=%fused_computation | loop fusion | flops 4096 | bytes 24576 | tf_op jit(solution)/shard_map/convert_element_type | solution.py:279

commit v2 on v1

v2 whole, which is shorter than its diff:
```python
import jax
import jax.numpy as jnp
from jax import lax
from jax.experimental import pallas as pl
from jax.experimental.pallas import tpu as pltpu
from jax.sharding import PartitionSpec as P

MESH = pl.DeviceIdType.MESH
SB = 8
XS, YS, ZS = 4, 4, 8
NCH = 4
LANES = 128
UPFRONT = True
DIRECT = (3,)
ORDER = list(zip("lambwdvambwdvamebwdvamebwdveeffffgggghhhhiiii", (0, 0, 0, 0, 0, 0, 0, 1, 1, 1, 1, 1, 1, 2, 2, 0, 2, 2, 2, 2, 3, 3, 1, 3, 3, 3, 3, 2, 3, 0, 1, 2, 3, 0, 1, 2, 3, 0, 1, 2, 3, 0, 1, 2, 3)))


def kernel(gamma, c_vir, c_occ, pairs, shells, out, g, cv, co, pair_s, shell_s,
           lw, rw, half, block, s_buf, r_d, r_1, r_2, r_3, c_buf, r_z,
           in_sem, send, recv):
    local, vir = g.shape
    basis = cv.shape[0]
    pair = lax.axis_index("pair")
    xlo = lax.axis_index("ao")
    core = lax.rem(pair, 2)
    y = lax.rem(lax.div(pair, 2), YS)
    z = lax.rem(lax.div(pair, 2 * YS), ZS)
    xhi = lax.div(pair, 2 * YS * ZS)
    yhi, ylo = lax.div(y, 2), lax.rem(y, 2)

    def device(xh, xl, yy, zz, cc):
        return (((xh * ZS + zz) * YS + yy) * 2 + cc, xl)

    def relative(hi, lo, a, b, c):
        own = lax.rem(hi + lo * (1 - c), 2)
        low = lax.rem(lo + b, 2)
        return lax.rem(own + a + low * (1 - c), 2), low

    def x_peer(a, b):
        hi, lo = relative(xhi, xlo, a, b, core)
        return device(hi, lo, y, z, core)

    def y_peer(a, b):
        hi, lo = relative(yhi, ylo, a, b, core)
        return device(xhi, xlo, hi * 2 + lo, z, core)

    def z_peer(dz):
        return device(xhi, xlo, y, lax.rem(z + dz, ZS), core)

    twin = device(xhi, xlo, y, z, 1 - core)
    x_first = device(lax.rem(xhi + core, 2), 1 - xlo, y, z, core)
    y_first = device(xhi, xlo, lax.rem(yhi + core, 2) * 2 + (1 - ylo), z, core)
    x_second = x_peer(0, 1)
    y_second = y_peer(0, 1)

    own_half = xlo * (basis // 2)
    other_half = (1 - xlo) * (basis // 2)

    def row_starts(j):
        return (pl.multiple_of(own_half + j * LANES, LANES), pl.multiple_of(other_half + j * LANES, LANES))

    mid = local // 2

    def load(src, dst, k):
        copy = pltpu.make_async_copy(src, dst, in_sem.at[k])
        copy.start()
        return copy

    def load_rows(j, k):
        for start in row_starts(j):
            load(c_vir.at[pl.ds(start, LANES)], cv.at[pl.ds(start, LANES)], k)

    def wait_rows(chunks, k):
        rows = cv.at[pl.ds(0, chunks * 2 * LANES)]
        pltpu.make_async_copy(rows, rows, in_sem.at[k]).wait()

    load_shells = load(shells, shell_s, 0)
    load_pairs = load(pairs, pair_s, 1)
    load_occ = load(c_occ, co, 2)
    load_rows(0, 3)
    load_gamma = [load(gamma.at[0, pl.ds(t * mid, mid)], g.at[pl.ds(t * mid, mid)], 4 + t) for t in range(2)]
    if UPFRONT:
        for k in range(1, NCH):
            load_rows(k, 6)

    barrier = pltpu.get_barrier_semaphore()
    peers = [twin]
    peers += [x_peer(a, b) for a, b in ((0, 1), (1, 0), (1, 1))]
    peers += [y_peer(a, b) for a, b in ((0, 1), (1, 0), (1, 1))]
    peers += [z_peer(dz) for dz in range(1, ZS)]
    for peer in peers:
        pl.semaphore_signal(barrier, inc=1, device_id=peer, device_id_type=MESH)

    load_shells.wait()
    bits = [(a, b) for a in range(2) for b in range(2)]
    z_part = [lax.rem(z + dz, ZS) * (2 * YS) for dz in range(ZS)]
    x_part, x_turn, y_part = {}, {}, {}
    for d in range(2):
        cc = lax.rem(core + d, 2)
        for e in range(2):
            x_part[d, e] = lax.rem(xhi + e, 2) * (2 * YS * ZS) + cc
            x_turn[d, e] = lax.rem(e + 1 - cc, 2)
        for a, b in bits:
            hi, lo = relative(yhi, ylo, a, b, cc)
            y_part[d, a, b] = (hi * 2 + lo) * 2

    def weights():
        load_pairs.wait()
        load_occ.wait()
        left = pair_s[0, pair]
        right = pair_s[1, pair]
        occ = co.shape[1]
        pick = jnp.where(lax.broadcasted_iota(jnp.int32, (occ, LANES), 0) == left, 1.0, 0.0).astype(jnp.bfloat16)
        lw[...] = jnp.dot(co[...], pick, preferred_element_type=jnp.float32).reshape(lw.shape)
        pick = jnp.where(lax.broadcasted_iota(jnp.int32, (16, occ), 1) == right, 1.0, 0.0).astype(jnp.bfloat16)
        rw[...] = lax.dot_general(pick, co[...], (((1,), (1,)), ((), ())), preferred_element_type=jnp.float32)[:8]

    def compute_half(j, t):
        rhs = jnp.concatenate([cv[pl.ds(start, LANES), :] for start in row_starts(j)], axis=0)
        half[pl.ds(t * mid, mid), :] = lax.dot_general(
            g[pl.ds(t * mid, mid), :], rhs, (((1,), (1,)), ((), ())), preferred_element_type=jnp.float32
        ).astype(jnp.bfloat16)

    def compute_block(j):
        column = pl.multiple_of(xlo * local, LANES)
        tall = basis // 2
        for t in range(2):
            block[pl.ds(t * tall // SB, tall // SB)] = jnp.dot(
                cv[pl.ds(t * tall, tall), pl.ds(column, local)], half[...], preferred_element_type=jnp.float32
            ).reshape(tall // SB, SB, 2 * LANES)

    def remote(src, dst, kind, j, peer):
        return pltpu.make_async_remote_copy(
            src_ref=src, dst_ref=dst, send_sem=send.at[kind], recv_sem=recv.at[kind, j], device_id=peer,
            device_id_type=MESH)

    def wait_all(ref, semaphore):
        pltpu.make_async_copy(ref, ref, semaphore).wait()

    def send_d(j):
        remote(s_buf.at[j, 1], r_d.at[j], 0, j, twin).start()

    def send_1(j, part):
        remote(s_buf.at[j, 0, part, pl.ds(32, 32)], r_1.at[j, part], 1, j, (x_first, y_first)[part]).start()

    def send_2(j, part):
        remote(s_buf.at[j, 0, part, pl.ds(16, 16)], r_2.at[j, part], 2, j, (x_second, y_second)[part]).start()

    def send_a(j, part, t):
        a, b = bits[t]
        kind, into = (2, r_2.at[j, part]) if t == 1 else (1, r_1.at[j, part, pl.ds((t - 2) * 16, 16)])
        remote(s_buf.at[j, 0, part, pl.ds(t * 16, 16)], into, kind, j, (x_peer if part == 0 else y_peer)(a, b)).start()

    def send_3(j, part, t):
        a, b = bits[t]
        remote(s_buf.at[j, 0, part, pl.ds(t * 4, 4)], r_3.at[j, part, t - 1], 3, j,
               (y_peer if part == 0 else x_peer)(a, b)).start()

    def send_z(j, dz):
        remote(c_buf.at[j, dz], r_z.at[j, dz - 1], 4, j, z_peer(dz)).start()

    def weigh(j, d):
        right = [rw[:, pl.ds(start, LANES)] for start in row_starts(j)]
        for part in range(2):
            for e in range(2):
                for v in range(4):
                    xy = x_part[d, e] + y_part[(d,) + bits[v]]
                    if part == 0:
                        own, other = e * 32 + v * 4, x_turn[d, e] * 32 + 16 + v * 4
                    else:
                        own, other = v * 16 + e * 8, x_turn[d, e] * 8 + v * 16 + 4
                    for w in range(4):
                        shell = shell_s[xy + z_part[part * 4 + w]]
                        left = lw[shell]
                        s_buf[j, d, part, own + w] = block[shell, :, 0:LANES] * right[0] * left
                        s_buf[j, d, part, other + w] = block[shell, :, LANES : 2 * LANES] * right[1] * left

    def stage_l(j):
        weights()
        wait_rows(1, 3)
        load_gamma[0].wait()
        if not UPFRONT:
            for k in range(1, NCH):
                load_rows(k, 6)

    def stage_a(j):
        compute_half(j, 0)

    def stage_m(j):
        if j == 0:
            load_gamma[1].wait()
        compute_half(j, 1)

    def stage_b(j):
        if j == 0:
            wait_rows(NCH - 1, 6)
        compute_block(j)

    def stage_w(j):
        weigh(j, 1)

    def stage_v(j):
        weigh(j, 0)

    def stage_d(j):
        if j == 0:
            pl.semaphore_wait(barrier, len(peers))
        send_d(j)

    def stage_e(j):
        wait_all(r_d.at[j], recv.at[0, j])
        direct = j in DIRECT
        first = 16 if direct else 32
        for part in range(2):
            rest = pl.ds(first, 64 - first)
            s_buf[j, 0, part, rest] = s_buf[j, 0, part, rest] + r_d[j, part, rest]
            if direct:
                for t in (3, 2, 1):
                    send_a(j, part, t)
            else:
                send_1(j, part)
        for part in range(2):
            kept = pl.ds(0, first)
            s_buf[j, 0, part, kept] = s_buf[j, 0, part, kept] + r_d[j, part, kept]

    def stage_f(j):
        if j in DIRECT:
            return
        wait_all(r_1.at[j], recv.at[1, j])
        for part in range(2):
            s_buf[j, 0, part, pl.ds(16, 16)] = s_buf[j, 0, part, pl.ds(16, 16)] + r_1[j, part, pl.ds(0, 16)]
            send_2(j, part)
        for part in range(2):
            s_buf[j, 0, part, pl.ds(0, 16)] = s_buf[j, 0, part, pl.ds(0, 16)] + r_1[j, part, pl.ds(16, 16)]

    def stage_g(j):
        if j in DIRECT:
            wait_all(r_1.at[j], recv.at[1, j])
        wait_all(r_2.at[j], recv.at[2, j])
        for part in range(2):
            total = s_buf[j, 0, part, pl.ds(0, 16)] + r_2[j, part]
            if j in DIRECT:
                total = total + r_1[j, part, pl.ds(0, 16)] + r_1[j, part, pl.ds(16, 16)]
            s_buf[j, 0, part, pl.ds(0, 16)] = total
            for t in (3, 2, 1):
                send_3(j, part, t)

    def stage_h(j):
        wait_all(r_3.at[j], recv.at[3, j])
        for part in range(2):
            total = s_buf[j, 0, part, pl.ds(0, 4)]
            for t in range(3):
                total = total + r_3[j, part, t]
            c_buf[j, pl.ds(part * 4, 4)] = total
        for dz in (4, 3, 5, 2, 6, 1, 7):
            send_z(j, dz)

    def stage_i(j):
        wait_all(r_z.at[j], recv.at[4, j])
        total = c_buf[j, 0]
        for dz in range(1, ZS):
            total = total + r_z[j, dz - 1]
        out[:, j * LANES : (j + 1) * LANES] = total

    stages = dict(l=stage_l, a=stage_a, m=stage_m, b=stage_b, w=stage_w, v=stage_v, d=stage_d,
                  e=stage_e, f=stage_f, g=stage_g, h=stage_h, i=stage_i)
    for name, j in ORDER:
        stages[name](j)
    for kind, ref in enumerate((r_d, r_1, r_2, r_3, r_z)):
        wait_all(ref, send.at[kind])


def shards(gamma, c_vir, c_occ, pair_list, shell_order):
    local, vir = gamma.shape[1:]
    basis = c_vir.shape[0]
    f32, bf16 = jnp.float32, jnp.bfloat16
    dma = pltpu.SemaphoreType.DMA
    tile = (SB, LANES)
    summed = pl.pallas_call(
        kernel,
        out_shape=jax.ShapeDtypeStruct((SB, basis // 2), f32),
        in_specs=[pl.BlockSpec(memory_space=pl.ANY)] * 5,
        out_specs=pl.BlockSpec(memory_space=pltpu.VMEM),
        scratch_shapes=[
            pltpu.VMEM((local, vir), bf16),
            pltpu.VMEM((basis, vir), bf16),
            pltpu.VMEM(c_occ.shape, bf16),
            pltpu.SMEM((2, pair_list.shape[0]), jnp.int32),
            pltpu.SMEM(shell_order.shape, jnp.int32),
            pltpu.VMEM((basis // SB, SB, LANES), f32),
            pltpu.VMEM((8, basis), f32),
            pltpu.VMEM((local, 2 * LANES), bf16),
            pltpu.VMEM((basis // SB, SB, 2 * LANES), f32),
            pltpu.VMEM((NCH, 2, 2, 64) + tile, f32),
            pltpu.VMEM((NCH, 2, 64) + tile, f32),
            pltpu.VMEM((NCH, 2, 32) + tile, f32),
            pltpu.VMEM((NCH, 2, 16) + tile, f32),
            pltpu.VMEM((NCH, 2, 3, 4) + tile, f32),
            pltpu.VMEM((NCH, ZS) + tile, f32),
            pltpu.VMEM((NCH, ZS - 1) + tile, f32),
            dma((7,)),
            dma((5,)),
            dma((5, NCH)),
        ],
        compiler_params=pltpu.CompilerParams(
            collective_id=0, has_side_effects=True, vmem_limit_bytes=60 * 1024 * 1024),
        name="density",
    )(gamma, c_vir, c_occ, pair_list.T, shell_order)
    return summed.T.astype(bf16)


def solution(mesh):
    return jax.shard_map(
        shards,
        mesh=mesh,
        in_specs=(P("pair", "ao", None), P(), P(), P(), P()),
        out_specs=P("ao", "pair"),
        check_vma=False,
    )
```

time: 40.6 us -> 36.9 us (0.909)
  the two profiles are of different devices: /device:TPU:32 before, /device:TPU:1 now
where the time goes in v2:
time: 36.9 us; the launch traced here: 36.6 us
  Pallas kernels  35.3 us (96%)
  other arithmetic  1.32 us (4%)
    pallas_call x1, Pallas kernels, shards(): pl.pallas_call(kernel, out_shape=jax.ShapeDtypeStruct((SB, basis // 2), f...  35.3 us
    convert_element_type x1, other arithmetic, shards(): return summed.T.astype(bf16)  1.32 us

profile of v2, /device:TPU:1, one launch (start us, length us, event | category | flops | bytes accessed | tf_op | source)
XLA Modules:
  0.0 36.6 jit_solution(319638433060085456)
XLA Ops:
  0.0 35.3 %density.1 = f32[8,512]{1,0:T(8,128)} custom-call(bf16[1,896,1792]{2,1,0:T(8,128)(2,1)} %gamma.1, bf16[1024,1792]{1,0:T(8,128)(2,1)} %c_vir.1, bf16[1024,256]{1,0:T(8,128)(2,1)} %c_occ.1, s32[2,128]{1,0:T(2,128)} %bitcast.3, s32[128]{0:T(128)} %shells.1), custom_call_target="tpu_custom_call" | custom-call | tf_op jit(solution)/shard_map/density/pallas_call | solution.py:279
  35.3 1.3 %convert_bitcast_fusion = bf16[512,8]{0,1:T(8,128)(2,1)} fusion(f32[8,512]{1,0:T(8,128)} %density.1), kind=kLoop, calls=%fused_computation | loop fusion | flops 4096 | bytes 24576 | tf_op jit(solution)/shard_map/convert_element_type | solution.py:309

commit v3 on v2

--- a/solution.py
+++ b/solution.py
@@ -10,9 +10,8 @@
 XS, YS, ZS = 4, 4, 8
 NCH = 4
 LANES = 128
-UPFRONT = True
 DIRECT = (3,)
-ORDER = list(zip("lambwdvambwdvamebwdvamebwdveeffffgggghhhhiiii", (0, 0, 0, 0, 0, 0, 0, 1, 1, 1, 1, 1, 1, 2, 2, 0, 2, 2, 2, 2, 3, 3, 1, 3, 3, 3, 3, 2, 3, 0, 1, 2, 3, 0, 1, 2, 3, 0, 1, 2, 3, 0, 1, 2, 3)))
+ORDER = list(zip("lambwdvambwdvamebwdvamebwdveefffgggghhhhiiii", (0, 0, 0, 0, 0, 0, 0, 1, 1, 1, 1, 1, 1, 2, 2, 0, 2, 2, 2, 2, 3, 3, 1, 3, 3, 3, 3, 2, 3, 0, 1, 2, 0, 1, 3, 2, 0, 1, 3, 2, 0, 1, 3, 2)))
 
 
 def kernel(gamma, c_vir, c_occ, pairs, shells, out, g, cv, co, pair_s, shell_s,
@@ -79,9 +78,8 @@
     load_occ = load(c_occ, co, 2)
     load_rows(0, 3)
     load_gamma = [load(gamma.at[0, pl.ds(t * mid, mid)], g.at[pl.ds(t * mid, mid)], 4 + t) for t in range(2)]
-    if UPFRONT:
-        for k in range(1, NCH):
-            load_rows(k, 6)
+    for k in range(1, NCH):
+        load_rows(k, 6)
 
     barrier = pltpu.get_barrier_semaphore()
     peers = [twin]
@@ -179,9 +177,6 @@
         weights()
         wait_rows(1, 3)
         load_gamma[0].wait()
-        if not UPFRONT:
-            for k in range(1, NCH):
-                load_rows(k, 6)
 
     def stage_a(j):
         compute_half(j, 0)
@@ -215,7 +210,7 @@
             rest = pl.ds(first, 64 - first)
             s_buf[j, 0, part, rest] = s_buf[j, 0, part, rest] + r_d[j, part, rest]
             if direct:
-                for t in (3, 2, 1):
+                for t in (2, 1, 3):
                     send_a(j, part, t)
             else:
                 send_1(j, part)
@@ -242,7 +237,7 @@
             if j in DIRECT:
                 total = total + r_1[j, part, pl.ds(0, 16)] + r_1[j, part, pl.ds(16, 16)]
             s_buf[j, 0, part, pl.ds(0, 16)] = total
-            for t in (3, 2, 1):
+            for t in (2, 1, 3):
                 send_3(j, part, t)
 
     def stage_h(j):

time: 36.9 us -> 36.7 us (level)
  no operation moved by 1% of the time
where the time goes in v3:
time: 36.7 us; the launch traced here: 36.5 us
  Pallas kernels  35.2 us (96%)
  other arithmetic  1.32 us (4%)
    pallas_call x1, Pallas kernels, shards(): pl.pallas_call(kernel, out_shape=jax.ShapeDtypeStruct((SB, basis // 2), f...  35.2 us
    convert_element_type x1, other arithmetic, shards(): return summed.T.astype(bf16)  1.32 us

profile of v3, /device:TPU:1, one launch (start us, length us, event | category | flops | bytes accessed | tf_op | source)
XLA Modules:
  0.0 36.5 jit_solution(12228782435443070333)
XLA Ops:
  0.0 35.2 %density.1 = f32[8,512]{1,0:T(8,128)} custom-call(bf16[1,896,1792]{2,1,0:T(8,128)(2,1)} %gamma.1, bf16[1024,1792]{1,0:T(8,128)(2,1)} %c_vir.1, bf16[1024,256]{1,0:T(8,128)(2,1)} %c_occ.1, s32[2,128]{1,0:T(2,128)} %bitcast.3, s32[128]{0:T(128)} %shells.1), custom_call_target="tpu_custom_call" | custom-call | tf_op jit(solution)/shard_map/density/pallas_call | solution.py:274
  35.2 1.3 %convert_bitcast_fusion = bf16[512,8]{0,1:T(8,128)(2,1)} fusion(f32[8,512]{1,0:T(8,128)} %density.1), kind=kLoop, calls=%fused_computation | loop fusion | flops 4096 | bytes 24576 | tf_op jit(solution)/shard_map/convert_element_type | solution.py:304

commit v4 on v3

--- a/solution.py
+++ b/solution.py
@@ -11,7 +11,7 @@
 NCH = 4
 LANES = 128
 DIRECT = (3,)
-ORDER = list(zip("lambwdvambwdvamebwdvamebwdveefffgggghhhhiiii", (0, 0, 0, 0, 0, 0, 0, 1, 1, 1, 1, 1, 1, 2, 2, 0, 2, 2, 2, 2, 3, 3, 1, 3, 3, 3, 3, 2, 3, 0, 1, 2, 0, 1, 3, 2, 0, 1, 3, 2, 0, 1, 3, 2)))
+ORDER = list(zip("lambwdvambwdvamebwdvamebwdevefffgggghhhhi", (0, 0, 0, 0, 0, 0, 0, 1, 1, 1, 1, 1, 1, 2, 2, 0, 2, 2, 2, 2, 3, 3, 1, 3, 3, 3, 2, 3, 3, 0, 1, 2, 0, 1, 3, 2, 0, 1, 3, 2, 0)))
 
 
 def kernel(gamma, c_vir, c_occ, pairs, shells, out, g, cv, co, pair_s, shell_s,
@@ -129,7 +129,7 @@
 
     def remote(src, dst, kind, j, peer):
         return pltpu.make_async_remote_copy(
-            src_ref=src, dst_ref=dst, send_sem=send.at[kind], recv_sem=recv.at[kind, j], device_id=peer,
+            src_ref=src, dst_ref=dst, send_sem=send.at[kind], recv_sem=recv.at[kind * NCH + (j if kind < 4 else 0)], device_id=peer,
             device_id_type=MESH)
 
     def wait_all(ref, semaphore):
@@ -203,7 +203,7 @@
         send_d(j)
 
     def stage_e(j):
-        wait_all(r_d.at[j], recv.at[0, j])
+        wait_all(r_d.at[j], recv.at[0 * NCH + j])
         direct = j in DIRECT
         first = 16 if direct else 32
         for part in range(2):
@@ -221,7 +221,7 @@
     def stage_f(j):
         if j in DIRECT:
             return
-        wait_all(r_1.at[j], recv.at[1, j])
+        wait_all(r_1.at[j], recv.at[1 * NCH + j])
         for part in range(2):
             s_buf[j, 0, part, pl.ds(16, 16)] = s_buf[j, 0, part, pl.ds(16, 16)] + r_1[j, part, pl.ds(0, 16)]
             send_2(j, part)
@@ -230,8 +230,8 @@
 
     def stage_g(j):
         if j in DIRECT:
-            wait_all(r_1.at[j], recv.at[1, j])
-        wait_all(r_2.at[j], recv.at[2, j])
+            wait_all(r_1.at[j], recv.at[1 * NCH + j])
+        wait_all(r_2.at[j], recv.at[2 * NCH + j])
         for part in range(2):
             total = s_buf[j, 0, part, pl.ds(0, 16)] + r_2[j, part]
             if j in DIRECT:
@@ -241,7 +241,7 @@
                 send_3(j, part, t)
 
     def stage_h(j):
-        wait_all(r_3.at[j], recv.at[3, j])
+        wait_all(r_3.at[j], recv.at[3 * NCH + j])
         for part in range(2):
             total = s_buf[j, 0, part, pl.ds(0, 4)]
             for t in range(3):
@@ -251,11 +251,12 @@
             send_z(j, dz)
 
     def stage_i(j):
-        wait_all(r_z.at[j], recv.at[4, j])
-        total = c_buf[j, 0]
-        for dz in range(1, ZS):
-            total = total + r_z[j, dz - 1]
-        out[:, j * LANES : (j + 1) * LANES] = total
+        wait_all(r_z, recv.at[4 * NCH])
+        for k in range(NCH):
+            total = c_buf[k, 0]
+            for dz in range(1, ZS):
+                total = total + r_z[k, dz - 1]
+            out[:, k * LANES : (k + 1) * LANES] = total
 
     stages = dict(l=stage_l, a=stage_a, m=stage_m, b=stage_b, w=stage_w, v=stage_v, d=stage_d,
                   e=stage_e, f=stage_f, g=stage_g, h=stage_h, i=stage_i)
@@ -295,7 +296,7 @@
             pltpu.VMEM((NCH, ZS - 1) + tile, f32),
             dma((7,)),
             dma((5,)),
-            dma((5, NCH)),
+            dma((4 * NCH + 1,)),
         ],
         compiler_params=pltpu.CompilerParams(
             collective_id=0, has_side_effects=True, vmem_limit_bytes=60 * 1024 * 1024),

time: 36.7 us -> 36.7 us (level)
  no operation moved by 1% of the time
where the time goes in v4:
time: 36.7 us; the launch traced here: 36.5 us
  Pallas kernels  35.1 us (96%)
  other arithmetic  1.32 us (4%)
    pallas_call x1, Pallas kernels, shards(): pl.pallas_call(kernel, out_shape=jax.ShapeDtypeStruct((SB, basis // 2), f...  35.1 us
    convert_element_type x1, other arithmetic, shards(): return summed.T.astype(bf16)  1.32 us

profile of v4, /device:TPU:1, one launch (start us, length us, event | category | flops | bytes accessed | tf_op | source)
XLA Modules:
  0.0 36.5 jit_solution(13127226946104387653)
XLA Ops:
  0.0 35.1 %density.1 = f32[8,512]{1,0:T(8,128)} custom-call(bf16[1,896,1792]{2,1,0:T(8,128)(2,1)} %gamma.1, bf16[1024,1792]{1,0:T(8,128)(2,1)} %c_vir.1, bf16[1024,256]{1,0:T(8,128)(2,1)} %c_occ.1, s32[2,128]{1,0:T(2,128)} %bitcast.3, s32[128]{0:T(128)} %shells.1), custom_call_target="tpu_custom_call" | custom-call | tf_op jit(solution)/shard_map/density/pallas_call | solution.py:275
  35.1 1.3 %convert_bitcast_fusion = bf16[512,8]{0,1:T(8,128)(2,1)} fusion(f32[8,512]{1,0:T(8,128)} %density.1), kind=kLoop, calls=%fused_computation | loop fusion | flops 4096 | bytes 24576 | tf_op jit(solution)/shard_map/convert_element_type | solution.py:305
